TPU v7x, 32 devices: a whole 2x2x4 slice. The times are simulated.
32 devices in a mesh: expert: 4 (over y, core), shard: 8 (over z, x).
Axes of the slice: x: 2, y: 2, z: 4, core: 2. Of those that a mesh axis runs over, the one named last changes fastest.
Arguments:
- w_gate: float32 [128, 2048, 768], P('expert', 'shard'), may hold values from -0.1875 to 0.1875
- w_up: float32 [128, 2048, 768], P('expert', 'shard'), may hold values from -0.1875 to 0.1875
- router_weight: float32 [2048, 128], P('shard', 'expert'), may hold values from -0.125 to 0.125
- router_gain: float32 [2048], P('shard'), may hold values from 0.25 to 1.75
Outputs:
- serve_gate: bfloat16 [128, 2048, 768], P('expert', None, 'shard')
- serve_up: bfloat16 [128, 2048, 768], P('expert', None, 'shard')
- scale_gate: float32 [128, 768], P('expert', 'shard')
- scale_up: float32 [128, 768], P('expert', 'shard')
- serve_router: bfloat16 [2048, 128], replicated
All inputs are finite; a program needn't handle non-finite values. Where the computation divides by a largest or mean magnitude, that divisor is 1e-20 or more.
Results may differ from a plain program's by a relative error of at most 0.001.
Values may be sent and summed in bfloat16 or wider, within the bound.
A program may use at most 192 MiB of HBM per device.

v0:
```python
import jax
import jax.numpy as jnp
from jax import lax
from jax.sharding import PartitionSpec as P


def body(w_gate, w_up, router_weight, router_gain):
    scale_gate, scale_up = lax.pmax(
        (jnp.max(jnp.abs(w_gate), axis=1), jnp.max(jnp.abs(w_up), axis=1)), "shard"
    )
    narrow_gate, narrow_up = (
        (w_gate / jnp.expand_dims(scale_gate, 1)).astype(jnp.bfloat16),
        (w_up / jnp.expand_dims(scale_up, 1)).astype(jnp.bfloat16),
    )
    serve_gate, serve_up = (
        lax.all_to_all(narrow_gate, "shard", split_axis=2, concat_axis=1, tiled=True),
        lax.all_to_all(narrow_up, "shard", split_axis=2, concat_axis=1, tiled=True),
    )
    scale_gate = lax.dynamic_slice_in_dim(
        scale_gate, lax.axis_index("shard") * serve_gate.shape[2], serve_gate.shape[2], axis=1
    )
    scale_up = lax.dynamic_slice_in_dim(
        scale_up, lax.axis_index("shard") * serve_up.shape[2], serve_up.shape[2], axis=1
    )
    part_router = (router_weight * router_gain[:, None]).astype(jnp.bfloat16)
    row_router = lax.all_gather(part_router, "shard", axis=0, tiled=True)
    serve_router = lax.all_gather(row_router, "expert", axis=1, tiled=True)
    return (serve_gate, serve_up, scale_gate, scale_up, serve_router)


def solution(mesh):
    return jax.shard_map(
        body,
        mesh=mesh,
        in_specs=(
            P("expert", "shard", None),
            P("expert", "shard", None),
            P("shard", "expert"),
            P("shard"),
        ),
        out_specs=(
            P("expert", None, "shard"),
            P("expert", None, "shard"),
            P("expert", "shard"),
            P("expert", "shard"),
            P(),
        ),
        check_vma=False,
    )
```

profile of v0, /device:TPU:0, one launch (start us, length us, event | category | flops | bytes accessed | tf_op | source)
XLA Modules:
  0.0 771.9 jit_solution(16742101143083610115)
XLA Ops:
  7.2 0.0 all-reduce.3.cloned.1.call-start
  7.2 0.0 copy-start
  7.2 10.2 %abs_reduce_fusion = f32[32,768]{1,0:T(8,128)} fusion(f32[32,256,768]{2,1,0:T(8,128)} %param.5), kind=kLoop, calls=%fused_computation.1 | loop fusion | flops 12558336 | bytes 25264128 | tf_op jit(solution)/shard_map/reduce_max | solution.py:9
  17.4 5.3 copy-done
  22.7 3.0 abs_reduce_fusion.1
  25.7 0.0 all-reduce.3.cloned.1.call-update
  25.7 25.1 %copy.21 = f32[32,256,768]{1,0,2:T(8,128)} copy(f32[32,256,768]{2,1,0:T(8,128)} %param.4) | data formatting | bytes 50331648 | tf_op args[0]
  50.8 48.8 %all-reduce.3.cloned.1.call-done = (f32[32,768]{1,0:T(8,128)}, f32[32,768]{1,0:T(8,128)}) async-done(((f32[32,768]{1,0:T(8,128)}, f32[32,768]{1,0:T(8,128)}), (f32[32,768]{1,0:T(8,128)}, f32[32,768]{1,0:T(8,128)})) %all-reduce.3.cloned.1.call-update) | async-done | bytes 196624 | tf_op jit(solution)/shard_map/pmax | solution.py:8
  99.6 1.1 copy.20
  100.7 14.1 %divide_convert_fusion.1 = bf16[32,256,768]{1,0,2:T(8,128)(2,1)} fusion(f32[32,256,768]{1,0,2:T(8,128)} %copy.21, f32[32,768]{0,1:T(8,128)S(1)} %copy.20), kind=kLoop, calls=%fused_computation.2 | loop fusion | flops 12582912 | bytes 37847040 | tf_op jit(solution)/shard_map/convert_element_type | solution.py:12
  114.8 5.4 all-to-all-start
  120.2 0.0 copy-start.1
  120.2 25.1 %copy.25 = f32[32,256,768]{1,0,2:T(8,128)} copy(f32[32,256,768]{2,1,0:T(8,128)} %param.5) | data formatting | bytes 50331648 | tf_op args[1]
  145.3 0.0 copy-done.1
  145.3 0.2 copy.24
  145.5 0.0 copy-start.2
  145.5 0.0 copy-start.3
  145.5 14.1 %divide_convert_fusion = bf16[32,256,768]{1,0,2:T(8,128)(2,1)} fusion(f32[32,256,768]{1,0,2:T(8,128)} %copy.25, f32[32,768]{0,1:T(8,128)S(1)} %copy.24), kind=kLoop, calls=%fused_computation | loop fusion | flops 12582912 | bytes 37847040 | tf_op jit(solution)/shard_map/convert_element_type | solution.py:13
  159.6 231.8 %all-to-all-done = bf16[32,256,768]{1,0,2:T(8,128)(2,1)} async-done(((bf16[32,256,768]{1,0,2:T(8,128)(2,1)}), bf16[32,256,768]{1,0,2:T(8,128)(2,1)}, u32[]{:S(2)}, u32[]{:S(2)}) %all-to-all-start) | async-done | bytes 12582944 | tf_op jit(solution)/shard_map/all_to_all | solution.py:16
  391.4 5.3 all-to-all-start.1
  396.7 0.0 copy-done.2
  396.7 0.0 copy-done.3
  396.8 291.6 %all_gather.6 = bf16[2048,32]{0,1:T(8,128)(2,1)S(1)} all-gather(bf16[256,32]{0,1:T(8,128)(2,1)S(1)} %multiply_convert_fusion), channel_id=1, replica_groups=mesh['expert'=4,'shard'=8] {'shard'}, dimensions={0}, use_global_device_ids=true | all-gather | bytes 147456 | tf_op jit(solution)/shard_map/all_gather | solution.py:26
  688.4 7.1 all_gather.7
  695.5 1.0 copy.28
  696.5 1.4 constant_dynamic-slice_fusion
  698.0 14.1 %copy.23 = bf16[32,8,256,96]{2,1,3,0:T(8,128)(2,1)} copy(bf16[32,8,256,96]{2,0,3,1:T(8,128)(2,1)} %bitcast.2) | data formatting | bytes 25165824 | tf_op jit(solution)/shard_map/all_to_all | solution.py:16
  712.0 19.5 %all_to_all.29 = bf16[32,2048,96]{1,2,0:T(8,128)(2,1)} reshape(bf16[32,8,256,96]{2,1,3,0:T(8,128)(2,1)} %copy.23) | data formatting | bytes 25165824 | tf_op jit(solution)/shard_map/all_to_all | solution.py:16
  731.5 0.0 all-to-all-done.1
  731.5 14.1 %copy.27 = bf16[32,8,256,96]{2,1,3,0:T(8,128)(2,1)} copy(bf16[32,8,256,96]{2,0,3,1:T(8,128)(2,1)} %bitcast.5) | data formatting | bytes 25165824 | tf_op jit(solution)/shard_map/all_to_all | solution.py:17
  745.6 19.5 %all_to_all.33 = bf16[32,2048,96]{1,2,0:T(8,128)(2,1)} reshape(bf16[32,8,256,96]{2,1,3,0:T(8,128)(2,1)} %copy.27) | data formatting | bytes 25165824 | tf_op jit(solution)/shard_map/all_to_all | solution.py:17
  (1 shorter events, 0.0 us)
Async XLA Ops:
  7.2 92.4 %all-reduce.3.cloned.1.call-start = ((), (), s32[]{:S(2)}) async-start(), calls=%async_computation.2 | async-start | bytes 393216 | tf_op jit(solution)/shard_map/pmax | solution.py:8
  7.2 15.5 %copy-start = (f32[32,256,768]{2,1,0:T(8,128)S(1)}, f32[32,256,768]{2,1,0:T(8,128)}, u32[]{:S(2)}) copy-start(f32[32,256,768]{2,1,0:T(8,128)} %param.4) | copy-start | bytes 75497472
  114.8 276.6 %all-to-all-start = ((bf16[32,256,768]{1,0,2:T(8,128)(2,1)}), bf16[32,256,768]{1,0,2:T(8,128)(2,1)}, u32[]{:S(2)}, u32[]{:S(2)}) async-start(bf16[32,256,768]{1,0,2:T(8,128)(2,1)} %divide_convert_fusion.1), calls=%async_computation | async-start | bytes 25165824 | tf_op jit(solution)/shard_map/all_to_all | solution.py:16
  120.2 25.1 %copy-start.1 = (f32[32,768]{1,0:T(8,128)S(1)}, f32[32,768]{1,0:T(8,128)}, u32[]{:S(2)}) copy-start(f32[32,768]{1,0:T(8,128)} %get-tuple-element.11) | copy-start | bytes 294916
  145.5 251.3 %copy-start.2 = (f32[256,32]{0,1:T(8,128)S(1)}, f32[256,32]{0,1:T(8,128)}, u32[]{:S(2)}) copy-start(f32[256,32]{0,1:T(8,128)} %param.6) | copy-start | bytes 98308
  145.5 251.3 %copy-start.3 = (f32[256]{0:T(256)S(1)}, f32[256]{0:T(256)}, u32[]{:S(2)}) copy-start(f32[256]{0:T(256)} %param.7) | copy-start | bytes 3076
  391.4 340.1 %all-to-all-start.1 = ((bf16[32,256,768]{1,0,2:T(8,128)(2,1)}), bf16[32,256,768]{1,0,2:T(8,128)(2,1)}, u32[]{:S(2)}, u32[]{:S(2)}) async-start(bf16[32,256,768]{1,0,2:T(8,128)(2,1)} %divide_convert_fusion), calls=%async_computation.1 | async-start | bytes 25165824 | tf_op jit(solution)/shard_map/all_to_all | solution.py:17
Sparse Core Ops, SparseCore 0:
  25.9 73.6 all-reduce.2
where the time goes:
time: 774 us; the launch traced here: 772 us
  blocking collectives  299 us (39%)
  waiting for transfers between devices  281 us (36%)
  local copies, waits for them, and re-layouts  126 us (16%)
  other arithmetic  41.5 us (5%)
  between operations  14.1 us (2%)
  starting transfers between devices  10.8 us (1%)
    all_gather x1, blocking collectives, body(): row_router = lax.all_gather(part_router, 'shard', axis=0, tiled=True)  292 us
    all_to_all x1, waiting for transfers between devices, body(): lax.all_to_all(narrow_gate, 'shard', split_axis=2, concat_axis=1, tiled=T...  232 us
    unnamed x11, local copies, waits for them, and re-layouts  56.4 us
    pmax x1, waiting for transfers between devices, body(): lax.pmax((jnp.max(jnp.abs(w_gate), axis=1), jnp.max(jnp.abs(w_up), axis=1...  48.8 us
    all_to_all x2, local copies, waits for them, and re-layouts, body(): lax.all_to_all(narrow_up, 'shard', split_axis=2, concat_axis=1, tiled=True)  33.6 us
    all_to_all x2, local copies, waits for them, and re-layouts, body(): lax.all_to_all(narrow_gate, 'shard', split_axis=2, concat_axis=1, tiled=T...  33.5 us
  transfers between devices with their start and end apart: 3, of which 2 were waited for; matrix products, arithmetic and copies ran while one was open for 10% of the time, Pallas kernels for 0%

commit v1 on v0

--- a/solution.py
+++ b/solution.py
@@ -1,7 +1,24 @@
+import functools
 import jax
 import jax.numpy as jnp
 from jax import lax
 from jax.sharding import PartitionSpec as P
+
+
+def launch_the_axis_part(mat, which_dim, at_axis):
+    seen_now = jnp.concatenate(
+        jax.lax.all_to_all(
+            jnp.stack(jnp.split(mat, jax.lax.axis_size("shard"), axis=which_dim), axis=0),
+            "shard",
+            0,
+            0,
+        ),
+        axis=at_axis,
+    )
+    return seen_now
+
+
+move_the_levels_all = functools.partial(launch_the_axis_part, which_dim=2, at_axis=1)
 
 
 def body(w_gate, w_up, router_weight, router_gain):
@@ -13,7 +30,7 @@
         (w_up / jnp.expand_dims(scale_up, 1)).astype(jnp.bfloat16),
     )
     serve_gate, serve_up = (
-        lax.all_to_all(narrow_gate, "shard", split_axis=2, concat_axis=1, tiled=True),
+        move_the_levels_all(narrow_gate),
         lax.all_to_all(narrow_up, "shard", split_axis=2, concat_axis=1, tiled=True),
     )
     scale_gate = lax.dynamic_slice_in_dim(

time: 774 us -> 756 us (0.977)
  local copies, waits for them, and re-layouts: 126 us -> 112 us
    all_to_all x2 -> x0, local copies, waits for them, and re-layouts: 33.5 us -> none  [body(): lax.all_to_all(narrow_gate, 'shard', split_axis=2, concat_axis=1, tiled=T...]
    reshape x0 -> x1, local copies, waits for them, and re-layouts: none -> 10.9 us  [launch_the_axis_part(): jnp.concatenate(jax.lax.all_to_all(jnp.stack(jnp.split(mat, jax.lax.axis_...]
    unnamed x11 -> x18, local copies, waits for them, and re-layouts: 56.4 us -> 65 us
where the time goes in v1:
time: 756 us; the launch traced here: 755 us
  blocking collectives  299 us (40%)
  waiting for transfers between devices  281 us (37%)
  local copies, waits for them, and re-layouts  112 us (15%)
  other arithmetic  37.6 us (5%)
  between operations  14.1 us (2%)
  starting transfers between devices  10.8 us (1%)
    all_gather x1, blocking collectives, body(): row_router = lax.all_gather(part_router, 'shard', axis=0, tiled=True)  292 us
    all_to_all x1, waiting for transfers between devices, launch_the_axis_part(): jax.lax.all_to_all(jnp.stack(jnp.split(mat, jax.lax.axis_size('shard'), a...  232 us
    unnamed x18, local copies, waits for them, and re-layouts  65 us
    pmax x1, waiting for transfers between devices, body(): lax.pmax((jnp.max(jnp.abs(w_gate), axis=1), jnp.max(jnp.abs(w_up), axis=1...  49.2 us
    all_to_all x2, local copies, waits for them, and re-layouts, body(): lax.all_to_all(narrow_up, 'shard', split_axis=2, concat_axis=1, tiled=True)  33.6 us
  transfers between devices with their start and end apart: 3, of which 2 were waited for; matrix products, arithmetic and copies ran while one was open for 10% of the time, Pallas kernels for 0%

profile of v1, /device:TPU:0, one launch (start us, length us, event | category | flops | bytes accessed | tf_op | source)
XLA Modules:
  0.0 754.6 jit_solution(8349729934143389127)
XLA Ops:
  7.2 0.0 all-reduce.3.cloned.1.call-start
  7.2 0.0 copy-start
  7.2 10.2 %abs_reduce_fusion = f32[32,768]{1,0:T(8,128)} fusion(f32[32,256,768]{2,1,0:T(8,128)} %param.5), kind=kLoop, calls=%fused_computation.1 | loop fusion | flops 12558336 | bytes 25264128 | tf_op jit(solution)/shard_map/reduce_max | solution.py:26
  17.4 5.3 copy-done
  22.7 3.0 abs_reduce_fusion.1
  25.7 0.0 all-reduce.3.cloned.1.call-update
  25.7 24.7 %copy.25 = f32[32,256,768]{1,2,0:T(8,128)} copy(f32[32,256,768]{2,1,0:T(8,128)} %param.4) | data formatting | bytes 50331648 | tf_op args[0]
  50.4 49.2 %all-reduce.3.cloned.1.call-done = (f32[32,768]{1,0:T(8,128)}, f32[32,768]{1,0:T(8,128)}) async-done(((f32[32,768]{1,0:T(8,128)}, f32[32,768]{1,0:T(8,128)}), (f32[32,768]{1,0:T(8,128)}, f32[32,768]{1,0:T(8,128)})) %all-reduce.3.cloned.1.call-update) | async-done | bytes 196624 | tf_op jit(solution)/shard_map/pmax | solution.py:25
  99.6 10.3 %divide_convert_fusion.1 = bf16[32,256,768]{1,2,0:T(8,128)(2,1)S(1)} fusion(f32[32,256,768]{1,2,0:T(8,128)} %copy.25, f32[32,768]{1,0:T(8,128)} %get-tuple-element.15), kind=kLoop, calls=%fused_computation.2 | loop fusion | flops 12582912 | bytes 37847040 | tf_op jit(solution)/shard_map/convert_element_type | solution.py:29
  109.9 1.3 fusion.7
  111.2 1.3 fusion.6
  112.5 1.3 fusion.5
  113.8 1.3 fusion.4
  115.0 1.3 fusion.3
  116.3 1.3 fusion.2
  117.6 1.3 fusion.1
  118.9 1.3 fusion
  120.1 5.4 all-to-all-start
  125.6 0.0 copy-start.1
  125.6 25.1 %copy.28 = f32[32,256,768]{1,0,2:T(8,128)} copy(f32[32,256,768]{2,1,0:T(8,128)} %param.5) | data formatting | bytes 50331648 | tf_op args[1]
  150.6 0.0 copy-done.1
  150.6 0.2 copy.27
  150.8 14.1 %divide_convert_fusion = bf16[32,256,768]{1,0,2:T(8,128)(2,1)} fusion(f32[32,256,768]{1,0,2:T(8,128)} %copy.28, f32[32,768]{0,1:T(8,128)S(1)} %copy.27), kind=kLoop, calls=%fused_computation | loop fusion | flops 12582912 | bytes 37847040 | tf_op jit(solution)/shard_map/convert_element_type | solution.py:30
  164.9 0.0 copy-start.2
  164.9 0.0 copy-start.3
  164.9 231.8 %all-to-all-done = bf16[8,32,256,96]{2,3,1,0:T(8,128)(2,1)} async-done(((bf16[8,32,256,96]{2,3,1,0:T(8,128)(2,1)}), bf16[8,32,256,96]{2,3,1,0:T(8,128)(2,1)}, u32[]{:S(2)}, u32[]{:S(2)}) %all-to-all-start) | async-done | bytes 12582944 | tf_op jit(solution)/shard_map/all_to_all | solution.py:10
  396.7 5.3 all-to-all-start.1
  402.1 0.0 copy-done.2
  402.1 0.0 copy-done.3
  402.1 291.6 %all_gather.6 = bf16[2048,32]{0,1:T(8,128)(2,1)S(1)} all-gather(bf16[256,32]{0,1:T(8,128)(2,1)S(1)} %multiply_convert_fusion), channel_id=1, replica_groups=mesh['expert'=4,'shard'=8] {'shard'}, dimensions={0}, use_global_device_ids=true | all-gather | bytes 147456 | tf_op jit(solution)/shard_map/all_gather | solution.py:43
  693.7 7.1 all_gather.7
  700.9 1.0 copy.31
  701.9 1.4 constant_dynamic-slice_fusion
  703.3 10.9 %copy.33 = bf16[8,32,12,8,256]{4,3,0,2,1:T(8,128)(2,1)} copy(bf16[8,32,12,8,256]{4,3,2,1,0:T(8,128)(2,1)} %bitcast.12) | data formatting | bytes 25165824 | tf_op jit(solution)/shard_map/reshape | solution.py:9
  714.2 0.0 all-to-all-done.1
  714.2 14.1 %copy.30 = bf16[32,8,256,96]{2,1,3,0:T(8,128)(2,1)} copy(bf16[32,8,256,96]{2,0,3,1:T(8,128)(2,1)} %bitcast.11) | data formatting | bytes 25165824 | tf_op jit(solution)/shard_map/all_to_all | solution.py:34
  728.3 19.5 %all_to_all.20 = bf16[32,2048,96]{1,2,0:T(8,128)(2,1)} reshape(bf16[32,8,256,96]{2,1,3,0:T(8,128)(2,1)} %copy.30) | data formatting | bytes 25165824 | tf_op jit(solution)/shard_map/all_to_all | solution.py:34
  (1 shorter events, 0.0 us)
Async XLA Ops:
  7.2 92.5 %all-reduce.3.cloned.1.call-start = ((), (), s32[]{:S(2)}) async-start(), calls=%async_computation.2 | async-start | bytes 393216 | tf_op jit(solution)/shard_map/pmax | solution.py:25
  7.2 15.5 %copy-start = (f32[32,256,768]{2,1,0:T(8,128)S(1)}, f32[32,256,768]{2,1,0:T(8,128)}, u32[]{:S(2)}) copy-start(f32[32,256,768]{2,1,0:T(8,128)} %param.4) | copy-start | bytes 75497472
  120.1 276.6 %all-to-all-start = ((bf16[8,32,256,96]{2,3,1,0:T(8,128)(2,1)}), bf16[8,32,256,96]{2,3,1,0:T(8,128)(2,1)}, u32[]{:S(2)}, u32[]{:S(2)}) async-start(bf16[8,32,256,96]{2,3,1,0:T(8,128)(2,1)} %fusion), calls=%async_computation | async-start | bytes 25165824 | tf_op jit(solution)/shard_map/all_to_all | solution.py:10
  125.6 25.1 %copy-start.1 = (f32[32,768]{1,0:T(8,128)S(1)}, f32[32,768]{1,0:T(8,128)}, u32[]{:S(2)}) copy-start(f32[32,768]{1,0:T(8,128)} %get-tuple-element.16) | copy-start | bytes 294916
  164.9 237.2 %copy-start.2 = (f32[256,32]{0,1:T(8,128)S(1)}, f32[256,32]{0,1:T(8,128)}, u32[]{:S(2)}) copy-start(f32[256,32]{0,1:T(8,128)} %param.6) | copy-start | bytes 98308
  164.9 237.2 %copy-start.3 = (f32[256]{0:T(256)S(1)}, f32[256]{0:T(256)}, u32[]{:S(2)}) copy-start(f32[256]{0:T(256)} %param.7) | copy-start | bytes 3076
  396.7 317.4 %all-to-all-start.1 = ((bf16[32,256,768]{1,0,2:T(8,128)(2,1)}), bf16[32,256,768]{1,0,2:T(8,128)(2,1)}, u32[]{:S(2)}, u32[]{:S(2)}) async-start(bf16[32,256,768]{1,0,2:T(8,128)(2,1)} %divide_convert_fusion), calls=%async_computation.1 | async-start | bytes 25165824 | tf_op jit(solution)/shard_map/all_to_all | solution.py:34
Sparse Core Ops, SparseCore 0:
  25.9 73.7 all-reduce.2
